TPU v7x, 8 devices: a whole 2x2x1 slice. The times are simulated.
8 devices in a mesh: dp: 2 (over y, z), tp: 4 (over x, core).
Axes of the slice: x: 2, y: 2, z: 1, core: 2. Of those that a mesh axis runs over, the one named last changes fastest.
Arguments:
- x: bfloat16 [4096, 2048], P(('dp', 'tp')), parts along dimension 0
- w_gate: bfloat16 [2048, 8192], P(None, 'tp')
- w_up: bfloat16 [2048, 8192], P(None, 'tp')
- w_down: bfloat16 [8192, 2048], P('tp')
Outputs:
- output: bfloat16 [4096, 2048], P(('dp', 'tp')), parts along dimension 0
There are 2 independent parts. A program takes and returns all parts, laid end to end along the dimension named above; an argument that names none is the same for every part.
All inputs are finite; a program needn't handle non-finite values.
Results may differ from a plain program's by a relative error of at most 0.016.
Values are sent between devices in bfloat16 or wider.
A program may use at most 2 GiB of HBM per device.

v0:
```python
import jax
import jax.numpy as jnp
from jax import lax
from jax.sharding import PartitionSpec as P


def solution(mesh):
    def step(x, w_gate, w_up, w_down):
        rows = lax.all_gather(x, "tp", axis=0, tiled=True)
        gate = jnp.dot(rows, w_gate, preferred_element_type=jnp.float32)
        up = jnp.dot(rows, w_up, preferred_element_type=jnp.float32)
        hidden = (jax.nn.silu(gate) * up).astype(jnp.bfloat16)
        term = jnp.dot(hidden, w_down, preferred_element_type=jnp.float32).astype(jnp.bfloat16)
        return lax.psum_scatter(term, "tp", scatter_dimension=0, tiled=True)

    return jax.shard_map(
        step,
        mesh=mesh,
        in_specs=(P(("dp", "tp"), None), P(None, "tp"), P(None, "tp"), P("tp", None)),
        out_specs=P(("dp", "tp"), None),
        check_vma=False,
    )
```

profile of v0, /device:TPU:1, one launch (start us, length us, event | category | flops | bytes accessed | tf_op | source)
XLA Modules:
  0.0 209.3 jit_solution(11728778351608449426)
XLA Ops:
  6.5 0.0 all-gather.2.cloned.1.call-start
  6.5 0.7 all-gather.2.cloned.1.call-update
  7.3 0.0 reduce-scatter.2.cloned.1.call-start
  7.3 59.5 %all-gather.2.cloned.1.call-done = bf16[2048,2048]{1,0:T(8,128)(2,1)} async-done(((bf16[512,2048]{1,0:T(8,128)(2,1)}), bf16[2048,2048]{1,0:T(8,128)(2,1)}) %all-gather.2.cloned.1.call-update) | async-done | bytes 8388624 | tf_op jit(solution)/shard_map/all_gather | solution.py:9
  66.8 0.0 copy-start.1
  66.8 24.5 %fusion.1 = f32[2048,2048]{1,0:T(8,128)} fusion(bf16[2048,2048]{1,0:T(8,128)(2,1)} %all-gather.2.cloned.1.call-done, bf16[2048,2048]{1,0:T(8,128)(2,1)} %param.5), kind=kOutput, calls=%fused_computation.3 | convolution fusion | flops 17179869184 | bytes 33554432 | tf_op jit(solution)/shard_map/dot_general | solution.py:10
  91.4 0.0 copy-done.1
  91.4 0.0 copy-start
  91.4 25.1 %multiply_convert_fusion.clone.4 = bf16[2048,2048]{1,0:T(8,128)(2,1)} fusion(f32[2048,2048]{1,0:T(8,128)} %fusion.1, bf16[2048,2048]{1,0:T(8,128)(2,1)S(1)} %copy-done.1, bf16[2048,2048]{1,0:T(8,128)(2,1)} %param.6), kind=kOutput, calls=%fused_computation.clone.clone.clone.1 | convolution fusion | flops 17205035008 | bytes 41943040 | tf_op jit(solution)/shard_map/dot_general | solution.py:11
  116.5 0.0 copy-done
  116.5 21.3 %convolution_convert_fusion = bf16[2048,2048]{1,0:T(8,128)(2,1)} fusion(bf16[2048,2048]{1,0:T(8,128)(2,1)S(1)} %copy-done, bf16[2048,2048]{1,0:T(8,128)(2,1)} %multiply_convert_fusion.clone.4), kind=kOutput, calls=%fused_computation.1 | convolution fusion | flops 17184063488 | bytes 25165824 | tf_op jit(solution)/shard_map/dot_general | solution.py:13
  137.8 0.0 reduce-scatter.2.cloned.1.call-update
  137.8 64.6 %reduce-scatter.2.cloned.1.call-done = bf16[512,2048]{1,0:T(8,128)(2,1)} async-done(((bf16[2048,2048]{1,0:T(8,128)(2,1)}), bf16[512,2048]{1,0:T(8,128)(2,1)}) %reduce-scatter.2.cloned.1.call-update) | async-done | bytes 2097168 | tf_op jit(solution)/shard_map/reduce_scatter | solution.py:14
Async XLA Ops:
  6.5 60.3 %all-gather.2.cloned.1.call-start = ((), (), s32[]{:S(2)}) async-start(), calls=%async_computation.1 | async-start | bytes 10485760 | tf_op jit(solution)/shard_map/all_gather | solution.py:9
  7.3 195.2 %reduce-scatter.2.cloned.1.call-start = ((), (), s32[]{:S(2)}) async-start(), calls=%async_computation.2 | async-start | bytes 10485760 | tf_op jit(solution)/shard_map/reduce_scatter | solution.py:14
  66.8 24.5 %copy-start.1 = (bf16[2048,2048]{1,0:T(8,128)(2,1)S(1)}, bf16[2048,2048]{1,0:T(8,128)(2,1)}, u32[]{:S(2)}) copy-start(bf16[2048,2048]{1,0:T(8,128)(2,1)} %all-gather.2.cloned.1.call-done) | copy-start | bytes 25165828
  91.4 25.1 %copy-start = (bf16[2048,2048]{1,0:T(8,128)(2,1)S(1)}, bf16[2048,2048]{1,0:T(8,128)(2,1)}, u32[]{:S(2)}) copy-start(bf16[2048,2048]{1,0:T(8,128)(2,1)} %param.7) | copy-start | bytes 25165828
Sparse Core Ops, SparseCore 0:
  8.9 57.9 all-gather.1
  138.0 64.4 reduce-scatter.1
where the time goes:
time: 211 us; the launch traced here: 209 us
  waiting for transfers between devices  125 us (59%)
  matrix products  71 us (34%)
  between operations  13.4 us (6%)
    reduce_scatter x1, waiting for transfers between devices, step(): return lax.psum_scatter(term, 'tp', scatter_dimension=0, tiled=True)  64.6 us
    all_gather x1, waiting for transfers between devices, step(): rows = lax.all_gather(x, 'tp', axis=0, tiled=True)  59.5 us
    dot_general x1, matrix products, step(): up = jnp.dot(rows, w_up, preferred_element_type=jnp.float32)  25.1 us
    dot_general x1, matrix products, step(): gate = jnp.dot(rows, w_gate, preferred_element_type=jnp.float32)  24.5 us
    dot_general x1, matrix products, step(): jnp.dot(hidden, w_down, preferred_element_type=jnp.float32)  21.3 us
  transfers between devices with their start and end apart: 2, of which 2 were waited for; matrix products, arithmetic and copies ran while one was open for 0% of the time, Pallas kernels for 0%

commit v1 on v0

v1 whole, which is shorter than its diff:
```python
import jax
import jax.numpy as jnp
from jax import lax
from jax.experimental import pallas as pl
from jax.experimental.pallas import tpu as pltpu
from jax.sharding import PartitionSpec as P

BF16, F32 = jnp.bfloat16, jnp.float32
MESH = pl.DeviceIdType.MESH

HALF = 128
M = 2 * HALF
NT = 512
BLK = 32

ORDER = (("L", 0), ("L", 1), ("L", 2), ("R", 0), ("R", 1), ("L", 3), ("R", 2), ("R", 3))
FORWARD_MID = {1: 0, 4: 2, 5: 3}
FORWARD_END = {2: 1}


def kernel(
    x, w_gate, w_up, w_down, out,
    xs, wg, wu, wd, hid, term, local, to_sib, from_sib, to_far, from_far, done,
    own_sem, w_sem, sib_send, sib_recv, far_send, far_recv, fwd_send, fwd_recv,
    term_send, term_recv, sum_send, sum_recv, out_sem,
):
    me = lax.axis_index("tp")
    sib = me + 1 - 2 * lax.rem(me, 2)
    far = lax.rem(me + 2, 4)
    steps = len(ORDER)
    tiles = wg.shape[0]
    dtiles = wd.shape[0]
    slot = {k: s for s, k in enumerate(ORDER)}
    chunks = x.shape[0] // HALF

    mine, other = pl.ds(0, HALF), pl.ds(HALF, HALF)

    def remote(src, dst, send, recv, tp):
        return pltpu.make_async_remote_copy(
            src_ref=src, dst_ref=dst, send_sem=send, recv_sem=recv,
            device_id={"tp": tp}, device_id_type=MESH)

    def own(j):
        return pltpu.make_async_copy(x.at[pl.ds(j * HALF, HALF)], xs.at[slot["L", j], mine], own_sem.at[j])

    def to_sibling(j):
        return remote(x.at[pl.ds(j * HALF, HALF)], xs.at[slot["L", j], other], sib_send.at[j], sib_recv.at[j], sib)

    def to_far_chip(j):
        return remote(x.at[pl.ds(j * HALF, HALF)], xs.at[slot["R", j], mine], far_send.at[j], far_recv.at[j], far)

    def forward(i):
        s = slot["R", i]
        return remote(xs.at[s, mine], xs.at[s, other], fwd_send.at[i], fwd_recv.at[i], sib)

    def term_copy(s):
        return remote(to_sib.at[s], from_sib.at[s], term_send.at[s], term_recv.at[s], sib)

    def sum_copy(i, b):
        rows = pl.ds(i * HALF + b * BLK, BLK)
        k = i * (HALF // BLK) + b
        return remote(to_far.at[rows], from_far.at[rows], sum_send.at[k], sum_recv.at[k], far)

    def weights(n):
        c = pl.ds(n * NT, NT)
        return (pltpu.make_async_copy(w_gate.at[:, c], wg.at[n], w_sem.at[0, n]),
                pltpu.make_async_copy(w_up.at[:, c], wu.at[n], w_sem.at[1, n]))

    def weights_down(n):
        return pltpu.make_async_copy(w_down.at[:, pl.ds(n * NT, NT)], wd.at[n], w_sem.at[2, n])

    def out_copy(i, b):
        rows = pl.ds(i * HALF + b * BLK, BLK)
        k = i * (HALF // BLK) + b
        return pltpu.make_async_copy(done.at[rows], out.at[rows], out_sem.at[k])

    barrier = pltpu.get_barrier_semaphore()
    for d in (sib, far):
        pl.semaphore_signal(barrier, inc=1, device_id={"tp": d}, device_id_type=MESH)
    own(0).start()
    for n in range(tiles):
        for c in weights(n):
            c.start()
    pl.semaphore_wait(barrier, 2)
    for j in range(chunks):
        to_far_chip(j).start()
    for j in range(chunks):
        to_sibling(j).start()
    for n in range(dtiles):
        weights_down(n).start()
    for j in range(1, chunks):
        own(j).start()

    def round_term(s):
        def blk(r, _):
            rows = pl.ds(pl.multiple_of(r * BLK, BLK), BLK)
            to_sib[s, rows] = term[lax.rem(s, 2), pl.ds(pl.multiple_of(HALF + r * BLK, BLK), BLK)].astype(BF16)
            return 0
        lax.fori_loop(0, HALF // BLK, blk, 0)

    def chip_sum(s):
        term_copy(s).wait_recv()
        kind, i = ORDER[s]

        def blk(r, _):
            rows = pl.ds(pl.multiple_of(r * BLK, BLK), BLK)
            both = term[s % 2, rows] + from_sib[s, rows].astype(F32)
            at = pl.ds(pl.multiple_of(i * HALF + r * BLK, BLK), BLK)
            if kind == "L":
                local[at] = both
            else:
                to_far[at] = both.astype(BF16)
            return 0
        lax.fori_loop(0, HALF // BLK, blk, 0)

    def start_sum(s):
        kind, i = ORDER[s]
        if kind == "R":
            for b in range(HALF // BLK):
                sum_copy(i, b).start()

    def step(s, _):
        for k, (kind, i) in enumerate(ORDER):
            @pl.when(s == k)
            def _():
                if kind == "L":
                    own(i).wait()
                    to_sibling(i).wait_recv()
                else:
                    forward(i).wait_recv()

        def gate_up(n, _):
            @pl.when(s == 0)
            def _():
                c = pl.ds(0, NT)
                pltpu.make_async_copy(w_gate.at[:, c], wg.at[n], w_sem.at[0, n]).wait()
                pltpu.make_async_copy(w_up.at[:, c], wu.at[n], w_sem.at[1, n]).wait()

            gate = jnp.dot(xs[s], wg[n], preferred_element_type=F32)
            up = jnp.dot(xs[s], wu[n], preferred_element_type=F32)
            hid[:, pl.ds(pl.multiple_of(n * NT, NT), NT)] = (jax.nn.silu(gate) * up).astype(BF16)

            @pl.when((n == 0) & (s > 0))
            def _():
                p = s - 1
                remote(to_sib.at[p], from_sib.at[p], term_send.at[p], term_recv.at[p], sib).start()
            return 0

        lax.fori_loop(0, tiles, gate_up, 0)

        for k, i in FORWARD_MID.items():
            @pl.when(s == k)
            def _():
                to_far_chip(i).wait_recv()
                forward(i).start()
        for k in range(1, steps):
            @pl.when(s == k)
            def _():
                chip_sum(k - 1)

        def down(n, _):
            @pl.when(s == 0)
            def _():
                pltpu.make_async_copy(w_down.at[:, pl.ds(0, NT)], wd.at[n], w_sem.at[2, n]).wait()

            cols = pl.ds(pl.multiple_of(n * NT, NT), NT)
            term[lax.rem(s, 2), :, cols] = jnp.dot(hid[...], wd[n], preferred_element_type=F32)
            return 0

        lax.fori_loop(0, dtiles, down, 0)

        round_term(s)
        for k, i in FORWARD_END.items():
            @pl.when(s == k)
            def _():
                to_far_chip(i).wait_recv()
                forward(i).start()
        for k in range(1, steps):
            if ORDER[k - 1][0] == "R":
                @pl.when(s == k)
                def _():
                    start_sum(k - 1)
        return 0

    lax.fori_loop(0, steps, step, 0)

    def finish(i, b):
        sum_copy(i, b).wait_recv()
        rows = pl.ds(i * HALF + b * BLK, BLK)
        done[rows] = (local[rows] + from_far[rows].astype(F32)).astype(BF16)
        out_copy(i, b).start()

    last = steps - 1
    term_copy(last).start()
    blocks = HALF // BLK
    for b in range(blocks):
        finish(0, b)
    chip_sum(last)
    for b in range(blocks):
        finish(1, b)
    start_sum(last)
    for i in range(2, chunks):
        for b in range(blocks):
            finish(i, b)

    for j in range(chunks):
        to_far_chip(j).wait_send()
        to_sibling(j).wait_send()
        forward(j).wait_send()
    for s in range(steps):
        term_copy(s).wait_send()
    for i in range(chunks):
        for b in range(blocks):
            sum_copy(i, b).wait_send()
            out_copy(i, b).wait()


def solution(mesh):
    def step(x, w_gate, w_up, w_down):
        rows, d = x.shape
        f = w_gate.shape[1]
        chunks = rows // HALF
        steps = len(ORDER)
        sums = chunks * (HALF // BLK)
        dma = pltpu.SemaphoreType.DMA
        return pl.pallas_call(
            kernel,
            out_shape=jax.ShapeDtypeStruct((rows, d), BF16),
            in_specs=[pl.BlockSpec(memory_space=pl.ANY)] * 4,
            out_specs=pl.BlockSpec(memory_space=pl.ANY),
            scratch_shapes=[
                pltpu.VMEM((steps, M, d), BF16),
                pltpu.VMEM((f // NT, d, NT), BF16),
                pltpu.VMEM((f // NT, d, NT), BF16),
                pltpu.VMEM((d // NT, f, NT), BF16),
                pltpu.VMEM((M, f), BF16),
                pltpu.VMEM((2, M, d), F32),
                pltpu.VMEM((rows, d), F32),
                pltpu.VMEM((steps, HALF, d), BF16),
                pltpu.VMEM((steps, HALF, d), BF16),
                pltpu.VMEM((rows, d), BF16),
                pltpu.VMEM((rows, d), BF16),
                pltpu.VMEM((rows, d), BF16),
                dma((chunks,)),
                dma((3, f // NT)),
                dma((chunks,)), dma((chunks,)),
                dma((chunks,)), dma((chunks,)),
                dma((chunks,)), dma((chunks,)),
                dma((steps,)), dma((steps,)),
                dma((sums,)), dma((sums,)),
                dma((sums,)),
            ],
            compiler_params=pltpu.CompilerParams(
                collective_id=0, has_side_effects=True, vmem_limit_bytes=67000000),
            name="mlp_ring",
        )(x, w_gate, w_up, w_down)

    return jax.shard_map(
        step,
        mesh=mesh,
        in_specs=(P(("dp", "tp"), None), P(None, "tp"), P(None, "tp"), P("tp", None)),
        out_specs=P(("dp", "tp"), None),
        check_vma=False,
    )
```

time: 211 us -> 101 us (0.48)
  waiting for transfers between devices: 125 us -> 0 us
  Pallas kernels: 0 us -> 96.4 us
  matrix products: 71 us -> 0 us
  between operations: 13.4 us -> 0.01 us
  local copies, waits for them, and re-layouts: 0.01 us -> 3.16 us
    pallas_call x0 -> x1, Pallas kernels: none -> 96.4 us  [step(): pl.pallas_call(kernel, out_shape=jax.ShapeDtypeStruct((rows, d), BF16), i...]
    dot_general x3 -> x0, matrix products: 71 us -> none  [the longest x1 25.1 us: step(): up = jnp.dot(rows, w_up, preferred_element_type=jnp.float32)]
    reduce_scatter x1 -> x0, waiting for transfers between devices: 64.6 us -> none  [step(): return lax.psum_scatter(term, 'tp', scatter_dimension=0, tiled=True)]
    all_gather x1 -> x0, waiting for transfers between devices: 59.5 us -> none  [step(): rows = lax.all_gather(x, 'tp', axis=0, tiled=True)]
    unnamed x4 -> x1, local copies, waits for them, and re-layouts: 0.01 us -> 3.16 us
  transfers between devices with their start and end apart: 2 -> 0, of which waited for: 2 -> 0; matrix products, arithmetic and copies ran while one was open for 0% -> 0% of each run, Pallas kernels for 0% -> 0%
where the time goes in v1:
time: 101 us; the launch traced here: 99.5 us
  Pallas kernels  96.4 us (95%)
  local copies, waits for them, and re-layouts  3.16 us (3%)
    pallas_call x1, Pallas kernels, step(): pl.pallas_call(kernel, out_shape=jax.ShapeDtypeStruct((rows, d), BF16), i...  96.4 us
    unnamed x1, local copies, waits for them, and re-layouts  3.16 us

profile of v1, /device:TPU:1, one launch (start us, length us, event | category | flops | bytes accessed | tf_op | source)
XLA Modules:
  0.0 99.5 jit_solution(2639183840918095740)
XLA Ops:
  0.0 96.4 %mlp_ring.1 = bf16[512,2048]{1,0:T(8,128)(2,1)} custom-call(bf16[512,2048]{1,0:T(8,128)(2,1)} %x.1, bf16[2048,2048]{1,0:T(8,128)(2,1)} %w_gate.1, bf16[2048,2048]{1,0:T(8,128)(2,1)} %w_up.1, bf16[2048,2048]{1,0:T(8,128)(2,1)} %w_down.1), custom_call_target="tpu_custom_call" | custom-call | tf_op jit(solution)/shard_map/mlp_ring/pallas_call | solution.py:226
  96.4 3.2 %copy.6 = bf16[512,2048]{1,0:T(8,128)(2,1)} copy(bf16[512,2048]{1,0:T(8,128)(2,1)} %mlp_ring.1) | data formatting | bytes 4194304

commit v2 on v1

--- a/solution.py
+++ b/solution.py
@@ -20,9 +20,9 @@
 
 def kernel(
     x, w_gate, w_up, w_down, out,
-    xs, wg, wu, wd, hid, term, local, to_sib, from_sib, to_far, from_far, done,
+    xs, wg, wu, wd, hid, term, local, to_sib, from_sib, to_far, from_far,
     own_sem, w_sem, sib_send, sib_recv, far_send, far_recv, fwd_send, fwd_recv,
-    term_send, term_recv, sum_send, sum_recv, out_sem,
+    term_send, term_recv, sum_send, sum_recv,
 ):
     me = lax.axis_index("tp")
     sib = me + 1 - 2 * lax.rem(me, 2)
@@ -44,10 +44,10 @@
         return pltpu.make_async_copy(x.at[pl.ds(j * HALF, HALF)], xs.at[slot["L", j], mine], own_sem.at[j])
 
     def to_sibling(j):
-        return remote(x.at[pl.ds(j * HALF, HALF)], xs.at[slot["L", j], other], sib_send.at[j], sib_recv.at[j], sib)
+        return remote(xs.at[slot["L", j], mine], xs.at[slot["L", j], other], sib_send.at[j], sib_recv.at[j], sib)
 
     def to_far_chip(j):
-        return remote(x.at[pl.ds(j * HALF, HALF)], xs.at[slot["R", j], mine], far_send.at[j], far_recv.at[j], far)
+        return remote(xs.at[slot["L", j], mine], xs.at[slot["R", j], mine], far_send.at[j], far_recv.at[j], far)
 
     def forward(i):
         s = slot["R", i]
@@ -77,19 +77,20 @@
     barrier = pltpu.get_barrier_semaphore()
     for d in (sib, far):
         pl.semaphore_signal(barrier, inc=1, device_id={"tp": d}, device_id_type=MESH)
-    own(0).start()
+    for j in range(chunks):
+        own(j).start()
+    for j in range(chunks):
+        own(j).wait()
+    pl.semaphore_wait(barrier, 2)
+    for j in range(chunks):
+        to_far_chip(j).start()
+    for j in range(chunks):
+        to_sibling(j).start()
     for n in range(tiles):
         for c in weights(n):
             c.start()
-    pl.semaphore_wait(barrier, 2)
-    for j in range(chunks):
-        to_far_chip(j).start()
-    for j in range(chunks):
-        to_sibling(j).start()
     for n in range(dtiles):
         weights_down(n).start()
-    for j in range(1, chunks):
-        own(j).start()
 
     def round_term(s):
         def blk(r, _):
@@ -124,7 +125,6 @@
             @pl.when(s == k)
             def _():
                 if kind == "L":
-                    own(i).wait()
                     to_sibling(i).wait_recv()
                 else:
                     forward(i).wait_recv()
@@ -187,8 +187,7 @@
     def finish(i, b):
         sum_copy(i, b).wait_recv()
         rows = pl.ds(i * HALF + b * BLK, BLK)
-        done[rows] = (local[rows] + from_far[rows].astype(F32)).astype(BF16)
-        out_copy(i, b).start()
+        out[rows] = (local[rows] + from_far[rows].astype(F32)).astype(BF16)
 
     last = steps - 1
     term_copy(last).start()
@@ -212,7 +211,6 @@
     for i in range(chunks):
         for b in range(blocks):
             sum_copy(i, b).wait_send()
-            out_copy(i, b).wait()
 
 
 def solution(mesh):
@@ -225,9 +223,9 @@
         dma = pltpu.SemaphoreType.DMA
         return pl.pallas_call(
             kernel,
-            out_shape=jax.ShapeDtypeStruct((rows, d), BF16),
+            out_shape=pltpu.VMEM((rows, d), BF16),
             in_specs=[pl.BlockSpec(memory_space=pl.ANY)] * 4,
-            out_specs=pl.BlockSpec(memory_space=pl.ANY),
+            out_specs=pl.BlockSpec(memory_space=pltpu.VMEM),
             scratch_shapes=[
                 pltpu.VMEM((steps, M, d), BF16),
                 pltpu.VMEM((f // NT, d, NT), BF16),
@@ -240,7 +238,6 @@
                 pltpu.VMEM((steps, HALF, d), BF16),
                 pltpu.VMEM((rows, d), BF16),
                 pltpu.VMEM((rows, d), BF16),
-                pltpu.VMEM((rows, d), BF16),
                 dma((chunks,)),
                 dma((3, f // NT)),
                 dma((chunks,)), dma((chunks,)),
@@ -248,10 +245,9 @@
                 dma((chunks,)), dma((chunks,)),
                 dma((steps,)), dma((steps,)),
                 dma((sums,)), dma((sums,)),
-                dma((sums,)),
             ],
             compiler_params=pltpu.CompilerParams(
-                collective_id=0, has_side_effects=True, vmem_limit_bytes=67000000),
+                collective_id=0, has_side_effects=True, vmem_limit_bytes=63000000),
             name="mlp_ring",
         )(x, w_gate, w_up, w_down)
 

time: 101 us -> 97.7 us (0.967)
  local copies, waits for them, and re-layouts: 3.16 us -> 1.32 us
  Pallas kernels: 96.4 us -> 94.8 us
    unnamed x1, local copies, waits for them, and re-layouts: 3.16 us -> 1.32 us
    pallas_call x1, Pallas kernels: 96.4 us -> 94.8 us  [step(): pl.pallas_call(kernel, out_shape=pltpu.VMEM((rows, d), BF16), in_specs=[p...]
where the time goes in v2:
time: 97.7 us; the launch traced here: 96.2 us
  Pallas kernels  94.8 us (97%)
  local copies, waits for them, and re-layouts  1.32 us (1%)
    pallas_call x1, Pallas kernels, step(): pl.pallas_call(kernel, out_shape=pltpu.VMEM((rows, d), BF16), in_specs=[p...  94.8 us

profile of v2, /device:TPU:1, one launch (start us, length us, event | category | flops | bytes accessed | tf_op | source)
XLA Modules:
  0.0 96.2 jit_solution(13290629964465062226)
XLA Ops:
  0.0 94.8 %mlp_ring.1 = bf16[512,2048]{1,0:T(8,128)(2,1)S(1)} custom-call(bf16[512,2048]{1,0:T(8,128)(2,1)} %x.1, bf16[2048,2048]{1,0:T(8,128)(2,1)} %w_gate.1, bf16[2048,2048]{1,0:T(8,128)(2,1)} %w_up.1, bf16[2048,2048]{1,0:T(8,128)(2,1)} %w_down.1), custom_call_target="tpu_custom_call" | custom-call | tf_op jit(solution)/shard_map/mlp_ring/pallas_call | solution.py:224
  94.8 1.3 %copy.6 = bf16[512,2048]{1,0:T(8,128)(2,1)} copy(bf16[512,2048]{1,0:T(8,128)(2,1)S(1)} %mlp_ring.1) | data formatting | bytes 4194304

commit v3 on v2

--- a/solution.py
+++ b/solution.py
@@ -12,19 +12,24 @@
 M = 2 * HALF
 NT = 512
 BLK = 32
-
-ORDER = (("L", 0), ("L", 1), ("L", 2), ("R", 0), ("R", 1), ("L", 3), ("R", 2), ("R", 3))
+MOVED = 32
+KEPT = HALF - MOVED
+PIECES = ((0, 0, HALF), (1, 0, HALF), (2, 0, HALF), (3, 0, KEPT), (3, KEPT, MOVED))
+
+ORDER = (("L", 0), ("L", 1), ("R", 0), ("L", 2), ("R", 1), ("R", 2), ("L", 3), ("R", 3))
 FORWARD_MID = {1: 0, 4: 2, 5: 3}
 FORWARD_END = {2: 1}
+LAST = 3
 
 
 def kernel(
     x, w_gate, w_up, w_down, out,
     xs, wg, wu, wd, hid, term, local, to_sib, from_sib, to_far, from_far,
     own_sem, w_sem, sib_send, sib_recv, far_send, far_recv, fwd_send, fwd_recv,
-    term_send, term_recv, sum_send, sum_recv,
+    extra_sem, term_send, term_recv, sum_send, sum_recv,
 ):
     me = lax.axis_index("tp")
+    core = lax.rem(me, 2)
     sib = me + 1 - 2 * lax.rem(me, 2)
     far = lax.rem(me + 2, 4)
     steps = len(ORDER)
@@ -46,20 +51,32 @@
     def to_sibling(j):
         return remote(xs.at[slot["L", j], mine], xs.at[slot["L", j], other], sib_send.at[j], sib_recv.at[j], sib)
 
-    def to_far_chip(j):
-        return remote(xs.at[slot["L", j], mine], xs.at[slot["R", j], mine], far_send.at[j], far_recv.at[j], far)
-
-    def forward(i):
+    def to_far_chip(p):
+        j, r, n = PIECES[p]
+        rows = pl.ds(r, n)
+        return remote(xs.at[slot["L", j], rows], xs.at[slot["R", j], rows], far_send.at[p], far_recv.at[p], far)
+
+    def forward(p):
+        i, r, n = PIECES[p]
         s = slot["R", i]
-        return remote(xs.at[s, mine], xs.at[s, other], fwd_send.at[i], fwd_recv.at[i], sib)
+        return remote(xs.at[s, pl.ds(r, n)], xs.at[s, pl.ds(HALF + r, n)], fwd_send.at[p], fwd_recv.at[p], sib)
+
+    moved = pl.ds(HALF + KEPT, MOVED)
+
+    def extra():
+        return remote(xs.at[slot["L", LAST], moved], xs.at[slot["R", LAST], moved], extra_sem.at[0], extra_sem.at[1], far)
+
+    def extra_forward():
+        s = slot["R", LAST]
+        return remote(xs.at[s, moved], xs.at[s, pl.ds(KEPT, MOVED)], extra_sem.at[2], extra_sem.at[3], sib)
 
     def term_copy(s):
         return remote(to_sib.at[s], from_sib.at[s], term_send.at[s], term_recv.at[s], sib)
 
-    def sum_copy(i, b):
-        rows = pl.ds(i * HALF + b * BLK, BLK)
-        k = i * (HALF // BLK) + b
-        return remote(to_far.at[rows], from_far.at[rows], sum_send.at[k], sum_recv.at[k], far)
+    def sum_copy(p):
+        i, r, n = PIECES[p]
+        rows = pl.ds(i * HALF + r, n)
+        return remote(to_far.at[rows], from_far.at[rows], sum_send.at[p], sum_recv.at[p], far)
 
     def weights(n):
         c = pl.ds(n * NT, NT)
@@ -68,27 +85,28 @@
 
     def weights_down(n):
         return pltpu.make_async_copy(w_down.at[:, pl.ds(n * NT, NT)], wd.at[n], w_sem.at[2, n])
-
-    def out_copy(i, b):
-        rows = pl.ds(i * HALF + b * BLK, BLK)
-        k = i * (HALF // BLK) + b
-        return pltpu.make_async_copy(done.at[rows], out.at[rows], out_sem.at[k])
 
     barrier = pltpu.get_barrier_semaphore()
     for d in (sib, far):
         pl.semaphore_signal(barrier, inc=1, device_id={"tp": d}, device_id_type=MESH)
     for j in range(chunks):
         own(j).start()
-    for j in range(chunks):
+    own(0).wait()
+    pl.semaphore_wait(barrier, 2)
+    to_far_chip(0).start()
+    for j in range(1, chunks):
         own(j).wait()
-    pl.semaphore_wait(barrier, 2)
-    for j in range(chunks):
         to_far_chip(j).start()
-    for j in range(chunks):
-        to_sibling(j).start()
+
+    @pl.when(core == 1)
+    def _():
+        to_far_chip(4).start()
+
     for n in range(tiles):
         for c in weights(n):
             c.start()
+    for j in range(chunks):
+        to_sibling(j).start()
     for n in range(dtiles):
         weights_down(n).start()
 
@@ -117,17 +135,35 @@
     def start_sum(s):
         kind, i = ORDER[s]
         if kind == "R":
-            for b in range(HALF // BLK):
-                sum_copy(i, b).start()
+            for p in range(len(PIECES)):
+                if PIECES[p][0] == i:
+                    sum_copy(p).start()
+
+    def pass_on(i):
+        to_far_chip(i).wait_recv()
+        forward(i).start()
+        if i == LAST:
+            @pl.when(core == 1)
+            def _():
+                to_far_chip(4).wait_recv()
+                forward(4).start()
+                extra().wait_recv()
+                extra_forward().start()
 
     def step(s, _):
         for k, (kind, i) in enumerate(ORDER):
             @pl.when(s == k)
             def _():
                 if kind == "L":
-                    to_sibling(i).wait_recv()
+                    if i != LAST:
+                        to_sibling(i).wait_recv()
                 else:
                     forward(i).wait_recv()
+                    if i == LAST:
+                        @pl.when(core == 0)
+                        def _():
+                            forward(4).wait_recv()
+                            extra_forward().wait_recv()
 
         def gate_up(n, _):
             @pl.when(s == 0)
@@ -148,11 +184,18 @@
 
         lax.fori_loop(0, tiles, gate_up, 0)
 
+        @pl.when(s == 0)
+        def _():
+            to_sibling(LAST).wait_recv()
+
+            @pl.when(core == 1)
+            def _():
+                extra().start()
+
         for k, i in FORWARD_MID.items():
             @pl.when(s == k)
             def _():
-                to_far_chip(i).wait_recv()
-                forward(i).start()
+                pass_on(i)
         for k in range(1, steps):
             @pl.when(s == k)
             def _():
@@ -165,6 +208,11 @@
 
             cols = pl.ds(pl.multiple_of(n * NT, NT), NT)
             term[lax.rem(s, 2), :, cols] = jnp.dot(hid[...], wd[n], preferred_element_type=F32)
+            for k in range(1, steps):
+                if ORDER[k - 1][0] == "R":
+                    @pl.when((n == 0) & (s == k))
+                    def _():
+                        start_sum(k - 1)
             return 0
 
         lax.fori_loop(0, dtiles, down, 0)
@@ -173,44 +221,42 @@
         for k, i in FORWARD_END.items():
             @pl.when(s == k)
             def _():
-                to_far_chip(i).wait_recv()
-                forward(i).start()
-        for k in range(1, steps):
-            if ORDER[k - 1][0] == "R":
-                @pl.when(s == k)
-                def _():
-                    start_sum(k - 1)
+                pass_on(i)
         return 0
 
     lax.fori_loop(0, steps, step, 0)
 
-    def finish(i, b):
-        sum_copy(i, b).wait_recv()
-        rows = pl.ds(i * HALF + b * BLK, BLK)
+    def finish(p):
+        sum_copy(p).wait_recv()
+        i, r, n = PIECES[p]
+        rows = pl.ds(i * HALF + r, n)
         out[rows] = (local[rows] + from_far[rows].astype(F32)).astype(BF16)
 
     last = steps - 1
+    finish(0)
     term_copy(last).start()
-    blocks = HALF // BLK
-    for b in range(blocks):
-        finish(0, b)
     chip_sum(last)
-    for b in range(blocks):
-        finish(1, b)
+    finish(1)
     start_sum(last)
-    for i in range(2, chunks):
-        for b in range(blocks):
-            finish(i, b)
+    for p in range(2, len(PIECES)):
+        finish(p)
 
     for j in range(chunks):
         to_far_chip(j).wait_send()
         to_sibling(j).wait_send()
         forward(j).wait_send()
+
+    @pl.when(core == 1)
+    def _():
+        to_far_chip(4).wait_send()
+        forward(4).wait_send()
+        extra().wait_send()
+        extra_forward().wait_send()
+
     for s in range(steps):
         term_copy(s).wait_send()
-    for i in range(chunks):
-        for b in range(blocks):
-            sum_copy(i, b).wait_send()
+    for p in range(len(PIECES)):
+        sum_copy(p).wait_send()
 
 
 def solution(mesh):
@@ -219,7 +265,7 @@
         f = w_gate.shape[1]
         chunks = rows // HALF
         steps = len(ORDER)
-        sums = chunks * (HALF // BLK)
+        pieces = len(PIECES)
         dma = pltpu.SemaphoreType.DMA
         return pl.pallas_call(
             kernel,
@@ -241,10 +287,11 @@
                 dma((chunks,)),
                 dma((3, f // NT)),
                 dma((chunks,)), dma((chunks,)),
-                dma((chunks,)), dma((chunks,)),
-                dma((chunks,)), dma((chunks,)),
+                dma((pieces,)), dma((pieces,)),
+                dma((pieces,)), dma((pieces,)),
+                dma((4,)),
                 dma((steps,)), dma((steps,)),
-                dma((sums,)), dma((sums,)),
+                dma((pieces,)), dma((pieces,)),
             ],
             compiler_params=pltpu.CompilerParams(
                 collective_id=0, has_side_effects=True, vmem_limit_bytes=63000000),

time: 97.7 us -> 96.1 us (0.984); the launches traced: 96.2 us -> 96 us
  no operation moved by 1% of the time
where the time goes in v3:
time: 96.1 us; the launch traced here: 96 us
  Pallas kernels  94.6 us (98%)
  local copies, waits for them, and re-layouts  1.32 us (1%)
    pallas_call x1, Pallas kernels, step(): pl.pallas_call(kernel, out_shape=pltpu.VMEM((rows, d), BF16), in_specs=[p...  94.6 us

profile of v3, /device:TPU:1, one launch (start us, length us, event | category | flops | bytes accessed | tf_op | source)
XLA Modules:
  0.0 96.0 jit_solution(12228820594160364147)
XLA Ops:
  0.0 94.6 %mlp_ring.1 = bf16[512,2048]{1,0:T(8,128)(2,1)S(1)} custom-call(bf16[512,2048]{1,0:T(8,128)(2,1)} %x.1, bf16[2048,2048]{1,0:T(8,128)(2,1)} %w_gate.1, bf16[2048,2048]{1,0:T(8,128)(2,1)} %w_up.1, bf16[2048,2048]{1,0:T(8,128)(2,1)} %w_down.1), custom_call_target="tpu_custom_call" | custom-call | tf_op jit(solution)/shard_map/mlp_ring/pallas_call | solution.py:270
  94.7 1.3 %copy.6 = bf16[512,2048]{1,0:T(8,128)(2,1)} copy(bf16[512,2048]{1,0:T(8,128)(2,1)S(1)} %mlp_ring.1) | data formatting | bytes 4194304

commit v4 on v3

--- a/solution.py
+++ b/solution.py
@@ -26,7 +26,7 @@
     x, w_gate, w_up, w_down, out,
     xs, wg, wu, wd, hid, term, local, to_sib, from_sib, to_far, from_far,
     own_sem, w_sem, sib_send, sib_recv, far_send, far_recv, fwd_send, fwd_recv,
-    extra_sem, term_send, term_recv, sum_send, sum_recv,
+    extra_sem, term_send, term_recv, sum_send, sum_recv, sib_in,
 ):
     me = lax.axis_index("tp")
     core = lax.rem(me, 2)
@@ -56,6 +56,9 @@
         rows = pl.ds(r, n)
         return remote(xs.at[slot["L", j], rows], xs.at[slot["R", j], rows], far_send.at[p], far_recv.at[p], far)
 
+    def first():
+        return remote(x.at[pl.ds(0, HALF)], xs.at[slot["R", 0], mine], far_send.at[0], far_recv.at[0], far)
+
     def forward(p):
         i, r, n = PIECES[p]
         s = slot["R", i]
@@ -87,16 +90,25 @@
         return pltpu.make_async_copy(w_down.at[:, pl.ds(n * NT, NT)], wd.at[n], w_sem.at[2, n])
 
     barrier = pltpu.get_barrier_semaphore()
-    for d in (sib, far):
-        pl.semaphore_signal(barrier, inc=1, device_id={"tp": d}, device_id_type=MESH)
+    pl.semaphore_signal(barrier, inc=1, device_id={"tp": far}, device_id_type=MESH)
+
+    @pl.when(core == 1)
+    def _():
+        pl.semaphore_signal(barrier, inc=1, device_id={"tp": sib}, device_id_type=MESH)
+
     for j in range(chunks):
         own(j).start()
-    own(0).wait()
-    pl.semaphore_wait(barrier, 2)
-    to_far_chip(0).start()
-    for j in range(1, chunks):
+    pl.semaphore_wait(barrier, 2 - core)
+    first().start()
+
+    @pl.when(core == 0)
+    def _():
+        pl.semaphore_signal(sib_in, inc=1, device_id={"tp": sib}, device_id_type=MESH)
+
+    for j in range(chunks):
         own(j).wait()
-        to_far_chip(j).start()
+        if j:
+            to_far_chip(j).start()
 
     @pl.when(core == 1)
     def _():
@@ -105,6 +117,11 @@
     for n in range(tiles):
         for c in weights(n):
             c.start()
+
+    @pl.when(core == 1)
+    def _():
+        pl.semaphore_wait(sib_in, 1)
+
     for j in range(chunks):
         to_sibling(j).start()
     for n in range(dtiles):
@@ -238,8 +255,7 @@
     chip_sum(last)
     finish(1)
     start_sum(last)
-    for p in range(2, len(PIECES)):
-        finish(p)
+    finish(2)
 
     for j in range(chunks):
         to_far_chip(j).wait_send()
@@ -255,7 +271,11 @@
 
     for s in range(steps):
         term_copy(s).wait_send()
-    for p in range(len(PIECES)):
+    for p in range(3):
+        sum_copy(p).wait_send()
+    for p in range(3, len(PIECES)):
+        finish(p)
+    for p in range(3, len(PIECES)):
         sum_copy(p).wait_send()
 
 
@@ -292,6 +312,7 @@
                 dma((4,)),
                 dma((steps,)), dma((steps,)),
                 dma((pieces,)), dma((pieces,)),
+                pltpu.SemaphoreType.REGULAR,
             ],
             compiler_params=pltpu.CompilerParams(
                 collective_id=0, has_side_effects=True, vmem_limit_bytes=63000000),

time: 96.1 us -> 95 us (0.989)
  Pallas kernels: 94.6 us -> 93.6 us
    pallas_call x1, Pallas kernels: 94.6 us -> 93.6 us  [step(): pl.pallas_call(kernel, out_shape=pltpu.VMEM((rows, d), BF16), in_specs=[p...]
where the time goes in v4:
time: 95 us; the launch traced here: 94.9 us
  Pallas kernels  93.6 us (99%)
  local copies, waits for them, and re-layouts  1.32 us (1%)
    pallas_call x1, Pallas kernels, step(): pl.pallas_call(kernel, out_shape=pltpu.VMEM((rows, d), BF16), in_specs=[p...  93.6 us

profile of v4, /device:TPU:1, one launch (start us, length us, event | category | flops | bytes accessed | tf_op | source)
XLA Modules:
  0.0 94.9 jit_solution(13066804955861790987)
XLA Ops:
  0.0 93.6 %mlp_ring.1 = bf16[512,2048]{1,0:T(8,128)(2,1)S(1)} custom-call(bf16[512,2048]{1,0:T(8,128)(2,1)} %x.1, bf16[2048,2048]{1,0:T(8,128)(2,1)} %w_gate.1, bf16[2048,2048]{1,0:T(8,128)(2,1)} %w_up.1, bf16[2048,2048]{1,0:T(8,128)(2,1)} %w_down.1), custom_call_target="tpu_custom_call" | custom-call | tf_op jit(solution)/shard_map/mlp_ring/pallas_call | solution.py:290
  93.6 1.3 %copy.6 = bf16[512,2048]{1,0:T(8,128)(2,1)} copy(bf16[512,2048]{1,0:T(8,128)(2,1)S(1)} %mlp_ring.1) | data formatting | bytes 4194304

commit v5 on v0

v5 whole, which is shorter than its diff:
```python
import jax
import jax.numpy as jnp
from jax import lax
from jax.experimental import pallas as pl
from jax.experimental.pallas import tpu as pltpu
from jax.sharding import PartitionSpec as P

BF16, F32 = jnp.bfloat16, jnp.float32
MESH = pl.DeviceIdType.MESH

HALF = 128
M = 2 * HALF
NT = 512
BLK = 32
MOVED = 32
KEPT = HALF - MOVED
PIECES = ((0, 0, HALF), (1, 0, HALF), (2, 0, HALF), (3, 0, KEPT), (3, KEPT, MOVED))
LAST = 3

ORDER = (("L", 0), ("L", 1), ("R", 0), ("L", 2), ("R", 1), ("R", 2), ("L", 3), ("R", 3))
SLOT = {k: s for s, k in enumerate(ORDER)}
FORWARD_MID = {1: 0, 4: 2, 5: 3}
FORWARD_END = {2: 1}
LOADS = ((0,), (1,), (2, 3))


def kernel(
    x, w_gate, w_up, w_down, out,
    xs, wgu, wd, hid, term, local, to_sib, from_sib, to_far, from_far,
    load, sib_recv, far_recv, fwd_recv, term_recv, sum_recv, send, sib_in,
):
    me = lax.axis_index("tp")
    core = lax.rem(me, 2)
    sib = me + 1 - 2 * core
    far = lax.rem(me + 2, 4)
    steps = len(ORDER)
    tiles = wd.shape[0]
    chunks = x.shape[0] // HALF
    to_far_sem, to_sib_sem, term_sem = send.at[0], send.at[1], send.at[2]

    def when(c, f):
        pl.when(c)(f)

    def remote(src, dst, send_sem, recv_sem, tp):
        return pltpu.make_async_remote_copy(
            src_ref=src, dst_ref=dst, send_sem=send_sem, recv_sem=recv_sem,
            device_id={"tp": tp}, device_id_type=MESH)

    def arrived(ref, sem):
        remote(ref, ref, sem, sem, far).wait_recv()

    def left(ref, sem):
        remote(ref, ref, sem, sem, far).wait_send()

    def slab(key, first, n):
        return xs.at[pl.ds(SLOT[key] * M + first, n)]

    def own(j):
        return pltpu.make_async_copy(x.at[pl.ds(j * HALF, HALF)], slab(("L", j), 0, HALF), load.at[0])

    def weights(n, sem):
        c = pl.ds(n * NT, NT)
        return (pltpu.make_async_copy(w_gate.at[:, c], wgu.at[2 * n], sem),
                pltpu.make_async_copy(w_up.at[:, c], wgu.at[2 * n + 1], sem))

    def weights_down(n):
        return pltpu.make_async_copy(w_down.at[:, pl.ds(n * NT, NT)], wd.at[n], load.at[len(LOADS)])

    def to_far_chip(p):
        j, r, n = PIECES[p]
        return remote(x.at[pl.ds(j * HALF + r, n)], slab(("R", j), r, n), to_far_sem, far_recv.at[j], far)

    def to_sibling(j):
        return remote(x.at[pl.ds(j * HALF, HALF)], slab(("L", j), HALF, HALF), to_sib_sem, sib_recv.at[min(j, 1)], sib)

    def forward(p):
        i, r, n = PIECES[p]
        return remote(slab(("R", i), r, n), slab(("R", i), HALF + r, n), to_sib_sem, fwd_recv.at[i], sib)

    def extra():
        return remote(slab(("L", LAST), HALF + KEPT, MOVED), slab(("R", LAST), HALF + KEPT, MOVED),
                      to_far_sem, far_recv.at[LAST], far)

    def extra_forward():
        return remote(slab(("R", LAST), HALF + KEPT, MOVED), slab(("R", LAST), KEPT, MOVED),
                      to_sib_sem, fwd_recv.at[LAST], sib)

    def term_copy(s):
        kind, i = ORDER[s]
        return remote(to_sib.at[s], from_sib.at[s], term_sem, term_recv.at[i if kind == "R" else chunks], sib)

    def sum_copy(p):
        i, r, n = PIECES[p]
        rows = pl.ds(i * HALF + r, n)
        return remote(to_far.at[rows], from_far.at[rows], to_far_sem, sum_recv.at[p // LAST_PIECE], far)

    barrier = pltpu.get_barrier_semaphore()
    pl.semaphore_signal(barrier, inc=1, device_id={"tp": far}, device_id_type=MESH)

    @pl.when(core == 1)
    def _():
        pl.semaphore_signal(barrier, inc=1, device_id={"tp": sib}, device_id_type=MESH)

    pl.semaphore_wait(barrier, 2 - core)
    for p in range(LAST_PIECE):
        to_far_chip(p).start()

    @pl.when(core == 0)
    def _():
        pl.semaphore_signal(sib_in, inc=1, device_id={"tp": sib}, device_id_type=MESH)

    @pl.when(core == 1)
    def _():
        to_far_chip(LAST_PIECE).start()

    for j in range(chunks):
        own(j).start()
    for k, group in enumerate(LOADS):
        for n in group:
            for c in weights(n, load.at[k]):
                c.start()

    @pl.when(core == 1)
    def _():
        pl.semaphore_wait(sib_in, 1)

    for j in range(chunks):
        to_sibling(j).start()
    for n in range(tiles):
        weights_down(n).start()

    def pass_on(i):
        if i != LAST:
            arrived(slab(("R", i), 0, HALF), far_recv.at[i])
            forward(i).start()
            return

        @pl.when(core == 0)
        def _():
            arrived(slab(("R", i), 0, KEPT), far_recv.at[i])
            forward(LAST).start()

        @pl.when(core == 1)
        def _():
            arrived(slab(("R", i), 0, HALF + MOVED), far_recv.at[i])
            forward(LAST).start()
            forward(LAST_PIECE).start()
            extra_forward().start()

    def rows_in(k):
        kind, i = ORDER[k]
        if kind == "L":
            if i == 0:
                arrived(slab(("L", 0), HALF, HALF), sib_recv.at[0])
        elif i != LAST:
            arrived(slab(("R", i), HALF, HALF), fwd_recv.at[i])
        else:
            @pl.when(core == 0)
            def _():
                arrived(slab(("R", i), 0, HALF + MOVED), fwd_recv.at[i])

            @pl.when(core == 1)
            def _():
                arrived(slab(("R", i), 0, KEPT), fwd_recv.at[i])

    def blocks(rows, f):
        def blk(r, _):
            f(pl.multiple_of(r * BLK, BLK))
            return 0
        lax.fori_loop(0, rows // BLK, blk, 0)

    def round_term(s):
        def blk(r):
            to_sib[s, pl.ds(r, BLK)] = term[lax.rem(s, 2), pl.ds(pl.multiple_of(HALF + r, BLK), BLK)].astype(BF16)
        blocks(HALF, blk)

    def keep_term(k):
        def blk(r):
            local[pl.ds(pl.multiple_of(ORDER[k][1] * HALF + r, BLK), BLK)] = term[k % 2, pl.ds(r, BLK)]
        blocks(HALF, blk)

    def add_sibling(j):
        def blk(r):
            at = pl.ds(pl.multiple_of(j * HALF + r, BLK), BLK)
            local[at] = local[at] + from_sib[SLOT["L", j], pl.ds(r, BLK)].astype(F32)
        blocks(HALF, blk)

    def chip_sum(k):
        i = ORDER[k][1]
        arrived(from_sib.at[k], term_recv.at[i])

        def blk(r):
            both = term[k % 2, pl.ds(r, BLK)] + from_sib[k, pl.ds(r, BLK)].astype(F32)
            to_far[pl.ds(pl.multiple_of(i * HALF + r, BLK), BLK)] = both.astype(BF16)
        blocks(HALF, blk)

    def start_sum(k):
        for p, (i, _, _) in enumerate(PIECES):
            if i == ORDER[k][1]:
                sum_copy(p).start()

    def step(s, _):
        for k in range(steps):
            when(s == k, lambda: rows_in(k))

        def gate_up(n, _):
            for k, group in enumerate(LOADS):
                count = 2 * len(group) + (1 if k == 0 else 0)
                when((s == 0) & (n == group[0]),
                     lambda: pltpu.make_async_copy(wgu.at[pl.ds(0, count)], wgu.at[pl.ds(0, count)], load.at[k]).wait())

            rows = xs.at[pl.ds(pl.multiple_of(s * M, M), M)]
            gate = jnp.dot(rows[...], wgu[2 * n], preferred_element_type=F32)
            up = jnp.dot(rows[...], wgu[2 * n + 1], preferred_element_type=F32)
            hid[:, pl.ds(pl.multiple_of(n * NT, NT), NT)] = (jax.nn.silu(gate) * up).astype(BF16)

            for k in range(1, steps):
                when((s == k) & (n == 0), lambda: term_copy(k - 1).start())
            return 0

        lax.fori_loop(0, tiles, gate_up, 0)

        @pl.when(s == 0)
        def _():
            pltpu.make_async_copy(wd, wd, load.at[len(LOADS)]).wait()
            arrived(xs.at[pl.ds(0, (chunks - 1) * HALF)], sib_recv.at[1])
            when(core == 1, lambda: extra().start())

        for k, i in FORWARD_MID.items():
            when(s == k, lambda: pass_on(i))
        for k in range(1, steps):
            if ORDER[k - 1][0] == "R":
                when(s == k, lambda: chip_sum(k - 1))

        def down(n, _):
            cols = pl.ds(pl.multiple_of(n * NT, NT), NT)
            term[lax.rem(s, 2), :, cols] = jnp.dot(hid[...], wd[n], preferred_element_type=F32)
            for k in range(1, steps):
                if ORDER[k - 1][0] == "R":
                    when((s == k) & (n == 0), lambda: start_sum(k - 1))
            return 0

        lax.fori_loop(0, tiles, down, 0)

        round_term(s)
        for k in range(steps):
            if ORDER[k][0] == "L":
                when(s == k, lambda: keep_term(k))
        for k, i in FORWARD_END.items():
            when(s == k, lambda: pass_on(i))
        return 0

    lax.fori_loop(0, steps, step, 0)

    last = steps - 1
    arrived(from_sib.at[pl.ds(0, chunks)], term_recv.at[chunks])
    add_sibling(0)
    add_sibling(1)
    term_copy(last).start()
    add_sibling(2)
    chip_sum(last)
    add_sibling(3)
    start_sum(last)

    def finish(p):
        i, r, n = PIECES[p]
        rows = pl.ds(i * HALF + r, n)
        out[rows] = (local[rows] + from_far[rows].astype(F32)).astype(BF16)

    left(to_sib, term_sem)
    sent = x.shape[0] - MOVED, x.shape[0] + MOVED
    for c in range(2):
        when(core == c, lambda: left(xs.at[pl.ds(0, x.shape[0] + sent[c])], to_sib_sem))
    arrived(from_far.at[pl.ds(0, x.shape[0] - MOVED)], sum_recv.at[0])
    for p in range(LAST_PIECE):
        finish(p)
    arrived(from_far.at[pl.ds(0, MOVED)], sum_recv.at[1])
    finish(LAST_PIECE)
    for c in range(2):
        when(core == c, lambda: left(xs.at[pl.ds(0, x.shape[0] + sent[c])], to_far_sem))


LAST_PIECE = len(PIECES) - 1


def solution(mesh):
    def step(x, w_gate, w_up, w_down):
        rows, d = x.shape
        f = w_gate.shape[1]
        chunks = rows // HALF
        steps = len(ORDER)
        dma = pltpu.SemaphoreType.DMA
        return pl.pallas_call(
            kernel,
            out_shape=pltpu.VMEM((rows, d), BF16),
            in_specs=[pl.BlockSpec(memory_space=pl.ANY)] * 4,
            out_specs=pl.BlockSpec(memory_space=pltpu.VMEM),
            scratch_shapes=[
                pltpu.VMEM((steps * M, d), BF16),
                pltpu.VMEM((2 * f // NT, d, NT), BF16),
                pltpu.VMEM((d // NT, f, NT), BF16),
                pltpu.VMEM((M, f), BF16),
                pltpu.VMEM((2, M, d), F32),
                pltpu.VMEM((rows, d), F32),
                pltpu.VMEM((steps, HALF, d), BF16),
                pltpu.VMEM((steps, HALF, d), BF16),
                pltpu.VMEM((rows, d), BF16),
                pltpu.VMEM((rows, d), BF16),
                dma((len(LOADS) + 1,)),
                dma((2,)),
                dma((chunks,)),
                dma((chunks,)),
                dma((chunks + 1,)),
                dma((2,)),
                dma((3,)),
                pltpu.SemaphoreType.REGULAR,
            ],
            compiler_params=pltpu.CompilerParams(
                collective_id=0, has_side_effects=True, vmem_limit_bytes=63000000),
            name="mlp_ring",
        )(x, w_gate, w_up, w_down)

    return jax.shard_map(
        step,
        mesh=mesh,
        in_specs=(P(("dp", "tp"), None), P(None, "tp"), P(None, "tp"), P("tp", None)),
        out_specs=P(("dp", "tp"), None),
        check_vma=False,
    )
```

time: 211 us -> 94.5 us (0.45)
  waiting for transfers between devices: 125 us -> 0 us
  Pallas kernels: 0 us -> 93.1 us
  matrix products: 71 us -> 0 us
  between operations: 13.4 us -> 0.01 us
    pallas_call x0 -> x1, Pallas kernels: none -> 93.1 us  [step(): pl.pallas_call(kernel, out_shape=pltpu.VMEM((rows, d), BF16), in_specs=[p...]
    dot_general x3 -> x0, matrix products: 71 us -> none  [the longest x1 25.1 us: step(): up = jnp.dot(rows, w_up, preferred_element_type=jnp.float32)]
    reduce_scatter x1 -> x0, waiting for transfers between devices: 64.6 us -> none  [step(): return lax.psum_scatter(term, 'tp', scatter_dimension=0, tiled=True)]
    all_gather x1 -> x0, waiting for transfers between devices: 59.5 us -> none  [step(): rows = lax.all_gather(x, 'tp', axis=0, tiled=True)]
  transfers between devices with their start and end apart: 2 -> 0, of which waited for: 2 -> 0; matrix products, arithmetic and copies ran while one was open for 0% -> 0% of each run, Pallas kernels for 0% -> 0%
where the time goes in v5:
time: 94.5 us
  Pallas kernels  93.1 us (99%)
  local copies, waits for them, and re-layouts  1.32 us (1%)
    pallas_call x1, Pallas kernels, step(): pl.pallas_call(kernel, out_shape=pltpu.VMEM((rows, d), BF16), in_specs=[p...  93.1 us

profile of v5, /device:TPU:1, one launch (start us, length us, event | category | flops | bytes accessed | tf_op | source)
XLA Modules:
  0.0 94.5 jit_solution(17076047871206850551)
XLA Ops:
  0.0 93.1 %mlp_ring.1 = bf16[512,2048]{1,0:T(8,128)(2,1)S(1)} custom-call(bf16[512,2048]{1,0:T(8,128)(2,1)} %x.1, bf16[2048,2048]{1,0:T(8,128)(2,1)} %w_gate.1, bf16[2048,2048]{1,0:T(8,128)(2,1)} %w_up.1, bf16[2048,2048]{1,0:T(8,128)(2,1)} %w_down.1), custom_call_target="tpu_custom_call" | custom-call | tf_op jit(solution)/shard_map/mlp_ring/pallas_call | solution.py:293
  93.1 1.3 %copy.6 = bf16[512,2048]{1,0:T(8,128)(2,1)} copy(bf16[512,2048]{1,0:T(8,128)(2,1)S(1)} %mlp_ring.1) | data formatting | bytes 4194304

commit v6 on v5

--- a/solution.py
+++ b/solution.py
@@ -27,7 +27,7 @@
 def kernel(
     x, w_gate, w_up, w_down, out,
     xs, wgu, wd, hid, term, local, to_sib, from_sib, to_far, from_far,
-    load, sib_recv, far_recv, fwd_recv, term_recv, sum_recv, send, sib_in,
+    load, early, far_recv, fwd_recv, own_term, sum_recv, sent, sib_in,
 ):
     me = lax.axis_index("tp")
     core = lax.rem(me, 2)
@@ -36,7 +36,11 @@
     steps = len(ORDER)
     tiles = wd.shape[0]
     chunks = x.shape[0] // HALF
-    to_far_sem, to_sib_sem, term_sem = send.at[0], send.at[1], send.at[2]
+    depth = x.shape[1]
+    sent = sent.at[0]
+    sib_recv = (early.at[0], early.at[1])
+    fwd_recv = (fwd_recv.at[0], fwd_recv.at[1], early.at[0], early.at[1])
+    term_recv = tuple(load.at[i] for i in range(4)) + (own_term.at[0],)
 
     def when(c, f):
         pl.when(c)(f)
@@ -60,39 +64,39 @@
 
     def weights(n, sem):
         c = pl.ds(n * NT, NT)
-        return (pltpu.make_async_copy(w_gate.at[:, c], wgu.at[2 * n], sem),
-                pltpu.make_async_copy(w_up.at[:, c], wgu.at[2 * n + 1], sem))
+        return (pltpu.make_async_copy(w_gate.at[:, c], wgu.at[pl.ds(2 * n * depth, depth)], sem),
+                pltpu.make_async_copy(w_up.at[:, c], wgu.at[pl.ds((2 * n + 1) * depth, depth)], sem))
 
     def weights_down(n):
         return pltpu.make_async_copy(w_down.at[:, pl.ds(n * NT, NT)], wd.at[n], load.at[len(LOADS)])
 
     def to_far_chip(p):
         j, r, n = PIECES[p]
-        return remote(x.at[pl.ds(j * HALF + r, n)], slab(("R", j), r, n), to_far_sem, far_recv.at[j], far)
+        return remote(x.at[pl.ds(j * HALF + r, n)], slab(("R", j), r, n), sent, far_recv.at[j], far)
 
     def to_sibling(j):
-        return remote(x.at[pl.ds(j * HALF, HALF)], slab(("L", j), HALF, HALF), to_sib_sem, sib_recv.at[min(j, 1)], sib)
+        return remote(x.at[pl.ds(j * HALF, HALF)], slab(("L", j), HALF, HALF), sent, sib_recv[min(j, 1)], sib)
 
     def forward(p):
         i, r, n = PIECES[p]
-        return remote(slab(("R", i), r, n), slab(("R", i), HALF + r, n), to_sib_sem, fwd_recv.at[i], sib)
+        return remote(slab(("R", i), r, n), slab(("R", i), HALF + r, n), sent, fwd_recv[i], sib)
 
     def extra():
         return remote(slab(("L", LAST), HALF + KEPT, MOVED), slab(("R", LAST), HALF + KEPT, MOVED),
-                      to_far_sem, far_recv.at[LAST], far)
+                      sent, far_recv.at[LAST], far)
 
     def extra_forward():
         return remote(slab(("R", LAST), HALF + KEPT, MOVED), slab(("R", LAST), KEPT, MOVED),
-                      to_sib_sem, fwd_recv.at[LAST], sib)
+                      sent, fwd_recv[LAST], sib)
 
     def term_copy(s):
         kind, i = ORDER[s]
-        return remote(to_sib.at[s], from_sib.at[s], term_sem, term_recv.at[i if kind == "R" else chunks], sib)
+        return remote(to_sib.at[s], from_sib.at[s], sent, term_recv[i if kind == "R" else chunks], sib)
 
     def sum_copy(p):
         i, r, n = PIECES[p]
         rows = pl.ds(i * HALF + r, n)
-        return remote(to_far.at[rows], from_far.at[rows], to_far_sem, sum_recv.at[p // LAST_PIECE], far)
+        return remote(to_far.at[rows], from_far.at[rows], sent, sum_recv.at[p // LAST_PIECE], far)
 
     barrier = pltpu.get_barrier_semaphore()
     pl.semaphore_signal(barrier, inc=1, device_id={"tp": far}, device_id_type=MESH)
@@ -151,17 +155,17 @@
         kind, i = ORDER[k]
         if kind == "L":
             if i == 0:
-                arrived(slab(("L", 0), HALF, HALF), sib_recv.at[0])
+                arrived(slab(("L", 0), HALF, HALF), sib_recv[0])
         elif i != LAST:
-            arrived(slab(("R", i), HALF, HALF), fwd_recv.at[i])
+            arrived(slab(("R", i), HALF, HALF), fwd_recv[i])
         else:
             @pl.when(core == 0)
             def _():
-                arrived(slab(("R", i), 0, HALF + MOVED), fwd_recv.at[i])
+                arrived(slab(("R", i), 0, HALF + MOVED), fwd_recv[i])
 
             @pl.when(core == 1)
             def _():
-                arrived(slab(("R", i), 0, KEPT), fwd_recv.at[i])
+                arrived(slab(("R", i), 0, KEPT), fwd_recv[i])
 
     def blocks(rows, f):
         def blk(r, _):
@@ -187,7 +191,7 @@
 
     def chip_sum(k):
         i = ORDER[k][1]
-        arrived(from_sib.at[k], term_recv.at[i])
+        arrived(from_sib.at[k], term_recv[i])
 
         def blk(r):
             both = term[k % 2, pl.ds(r, BLK)] + from_sib[k, pl.ds(r, BLK)].astype(F32)
@@ -207,11 +211,13 @@
             for k, group in enumerate(LOADS):
                 count = 2 * len(group) + (1 if k == 0 else 0)
                 when((s == 0) & (n == group[0]),
-                     lambda: pltpu.make_async_copy(wgu.at[pl.ds(0, count)], wgu.at[pl.ds(0, count)], load.at[k]).wait())
+                     lambda: pltpu.make_async_copy(
+                         wgu.at[pl.ds(0, count * depth)], wgu.at[pl.ds(0, count * depth)], load.at[k]).wait())
 
             rows = xs.at[pl.ds(pl.multiple_of(s * M, M), M)]
-            gate = jnp.dot(rows[...], wgu[2 * n], preferred_element_type=F32)
-            up = jnp.dot(rows[...], wgu[2 * n + 1], preferred_element_type=F32)
+            w = pl.multiple_of(2 * n * depth, depth)
+            gate = jnp.dot(rows[...], wgu[pl.ds(w, depth)], preferred_element_type=F32)
+            up = jnp.dot(rows[...], wgu[pl.ds(pl.multiple_of(w + depth, depth), depth)], preferred_element_type=F32)
             hid[:, pl.ds(pl.multiple_of(n * NT, NT), NT)] = (jax.nn.silu(gate) * up).astype(BF16)
 
             for k in range(1, steps):
@@ -223,14 +229,14 @@
         @pl.when(s == 0)
         def _():
             pltpu.make_async_copy(wd, wd, load.at[len(LOADS)]).wait()
-            arrived(xs.at[pl.ds(0, (chunks - 1) * HALF)], sib_recv.at[1])
+            arrived(xs.at[pl.ds(0, (chunks - 1) * HALF)], sib_recv[1])
             when(core == 1, lambda: extra().start())
 
-        for k, i in FORWARD_MID.items():
-            when(s == k, lambda: pass_on(i))
         for k in range(1, steps):
             if ORDER[k - 1][0] == "R":
                 when(s == k, lambda: chip_sum(k - 1))
+        for k, i in FORWARD_MID.items():
+            when(s == k, lambda: pass_on(i))
 
         def down(n, _):
             cols = pl.ds(pl.multiple_of(n * NT, NT), NT)
@@ -253,7 +259,7 @@
     lax.fori_loop(0, steps, step, 0)
 
     last = steps - 1
-    arrived(from_sib.at[pl.ds(0, chunks)], term_recv.at[chunks])
+    arrived(from_sib.at[pl.ds(0, chunks)], term_recv[chunks])
     add_sibling(0)
     add_sibling(1)
     term_copy(last).start()
@@ -267,17 +273,15 @@
         rows = pl.ds(i * HALF + r, n)
         out[rows] = (local[rows] + from_far[rows].astype(F32)).astype(BF16)
 
-    left(to_sib, term_sem)
-    sent = x.shape[0] - MOVED, x.shape[0] + MOVED
-    for c in range(2):
-        when(core == c, lambda: left(xs.at[pl.ds(0, x.shape[0] + sent[c])], to_sib_sem))
     arrived(from_far.at[pl.ds(0, x.shape[0] - MOVED)], sum_recv.at[0])
     for p in range(LAST_PIECE):
         finish(p)
     arrived(from_far.at[pl.ds(0, MOVED)], sum_recv.at[1])
     finish(LAST_PIECE)
-    for c in range(2):
-        when(core == c, lambda: left(xs.at[pl.ds(0, x.shape[0] + sent[c])], to_far_sem))
+    rows = x.shape[0]
+    for c, far_rows in enumerate((rows - MOVED, rows + MOVED)):
+        total = 2 * (far_rows + rows) + steps * HALF
+        when(core == c, lambda: left(wgu.at[pl.ds(0, total * x.shape[1] // NT)], sent))
 
 
 LAST_PIECE = len(PIECES) - 1
@@ -297,7 +301,7 @@
             out_specs=pl.BlockSpec(memory_space=pltpu.VMEM),
             scratch_shapes=[
                 pltpu.VMEM((steps * M, d), BF16),
-                pltpu.VMEM((2 * f // NT, d, NT), BF16),
+                pltpu.VMEM((2 * f // NT * d, NT), BF16),
                 pltpu.VMEM((d // NT, f, NT), BF16),
                 pltpu.VMEM((M, f), BF16),
                 pltpu.VMEM((2, M, d), F32),
@@ -309,10 +313,10 @@
                 dma((len(LOADS) + 1,)),
                 dma((2,)),
                 dma((chunks,)),
-                dma((chunks,)),
-                dma((chunks + 1,)),
                 dma((2,)),
-                dma((3,)),
+                dma((1,)),
+                dma((2,)),
+                dma((1,)),
                 pltpu.SemaphoreType.REGULAR,
             ],
             compiler_params=pltpu.CompilerParams(

time: 94.5 us -> 94.5 us (level)
  no operation moved by 1% of the time
where the time goes in v6:
time: 94.5 us; the launch traced here: 94.4 us
  Pallas kernels  93 us (98%)
  local copies, waits for them, and re-layouts  1.32 us (1%)
    pallas_call x1, Pallas kernels, step(): pl.pallas_call(kernel, out_shape=pltpu.VMEM((rows, d), BF16), in_specs=[p...  93 us

profile of v6, /device:TPU:1, one launch (start us, length us, event | category | flops | bytes accessed | tf_op | source)
XLA Modules:
  0.0 94.4 jit_solution(128690215040135505)
XLA Ops:
  0.0 93.0 %mlp_ring.1 = bf16[512,2048]{1,0:T(8,128)(2,1)S(1)} custom-call(bf16[512,2048]{1,0:T(8,128)(2,1)} %x.1, bf16[2048,2048]{1,0:T(8,128)(2,1)} %w_gate.1, bf16[2048,2048]{1,0:T(8,128)(2,1)} %w_up.1, bf16[2048,2048]{1,0:T(8,128)(2,1)} %w_down.1), custom_call_target="tpu_custom_call" | custom-call | tf_op jit(solution)/shard_map/mlp_ring/pallas_call | solution.py:297
  93.1 1.3 %copy.6 = bf16[512,2048]{1,0:T(8,128)(2,1)} copy(bf16[512,2048]{1,0:T(8,128)(2,1)S(1)} %mlp_ring.1) | data formatting | bytes 4194304

commit v7 on v6

--- a/solution.py
+++ b/solution.py
@@ -10,7 +10,7 @@
 
 HALF = 128
 M = 2 * HALF
-NT = 512
+NT = 1024
 BLK = 32
 MOVED = 32
 KEPT = HALF - MOVED
@@ -21,7 +21,6 @@
 SLOT = {k: s for s, k in enumerate(ORDER)}
 FORWARD_MID = {1: 0, 4: 2, 5: 3}
 FORWARD_END = {2: 1}
-LOADS = ((0,), (1,), (2, 3))
 
 
 def kernel(
@@ -40,7 +39,7 @@
     sent = sent.at[0]
     sib_recv = (early.at[0], early.at[1])
     fwd_recv = (fwd_recv.at[0], fwd_recv.at[1], early.at[0], early.at[1])
-    term_recv = tuple(load.at[i] for i in range(4)) + (own_term.at[0],)
+    term_recv = tuple(far_recv.at[i] for i in range(4)) + (own_term.at[0],)
 
     def when(c, f):
         pl.when(c)(f)
@@ -60,15 +59,15 @@
         return xs.at[pl.ds(SLOT[key] * M + first, n)]
 
     def own(j):
-        return pltpu.make_async_copy(x.at[pl.ds(j * HALF, HALF)], slab(("L", j), 0, HALF), load.at[0])
-
-    def weights(n, sem):
+        return pltpu.make_async_copy(x.at[pl.ds(j * HALF, HALF)], slab(("L", j), 0, HALF), sib_recv[0])
+
+    def weights(n):
         c = pl.ds(n * NT, NT)
-        return (pltpu.make_async_copy(w_gate.at[:, c], wgu.at[pl.ds(2 * n * depth, depth)], sem),
-                pltpu.make_async_copy(w_up.at[:, c], wgu.at[pl.ds((2 * n + 1) * depth, depth)], sem))
+        return (pltpu.make_async_copy(w_gate.at[:, c], wgu.at[pl.ds(2 * n * depth, depth)], load.at[0]),
+                pltpu.make_async_copy(w_up.at[:, c], wgu.at[pl.ds((2 * n + 1) * depth, depth)], load.at[0]))
 
     def weights_down(n):
-        return pltpu.make_async_copy(w_down.at[:, pl.ds(n * NT, NT)], wd.at[n], load.at[len(LOADS)])
+        return pltpu.make_async_copy(w_down.at[:, pl.ds(n * NT, NT)], wd.at[n], load.at[1])
 
     def to_far_chip(p):
         j, r, n = PIECES[p]
@@ -119,10 +118,9 @@
 
     for j in range(chunks):
         own(j).start()
-    for k, group in enumerate(LOADS):
-        for n in group:
-            for c in weights(n, load.at[k]):
-                c.start()
+    for n in range(tiles):
+        for c in weights(n):
+            c.start()
 
     @pl.when(core == 1)
     def _():
@@ -155,7 +153,8 @@
         kind, i = ORDER[k]
         if kind == "L":
             if i == 0:
-                arrived(slab(("L", 0), HALF, HALF), sib_recv[0])
+                arrived(xs.at[pl.ds(0, x.shape[0] + HALF)], sib_recv[0])
+                arrived(wgu, load.at[0])
         elif i != LAST:
             arrived(slab(("R", i), HALF, HALF), fwd_recv[i])
         else:
@@ -208,12 +207,6 @@
             when(s == k, lambda: rows_in(k))
 
         def gate_up(n, _):
-            for k, group in enumerate(LOADS):
-                count = 2 * len(group) + (1 if k == 0 else 0)
-                when((s == 0) & (n == group[0]),
-                     lambda: pltpu.make_async_copy(
-                         wgu.at[pl.ds(0, count * depth)], wgu.at[pl.ds(0, count * depth)], load.at[k]).wait())
-
             rows = xs.at[pl.ds(pl.multiple_of(s * M, M), M)]
             w = pl.multiple_of(2 * n * depth, depth)
             gate = jnp.dot(rows[...], wgu[pl.ds(w, depth)], preferred_element_type=F32)
@@ -228,7 +221,7 @@
 
         @pl.when(s == 0)
         def _():
-            pltpu.make_async_copy(wd, wd, load.at[len(LOADS)]).wait()
+            arrived(wd, load.at[1])
             arrived(xs.at[pl.ds(0, (chunks - 1) * HALF)], sib_recv[1])
             when(core == 1, lambda: extra().start())
 
@@ -310,7 +303,7 @@
                 pltpu.VMEM((steps, HALF, d), BF16),
                 pltpu.VMEM((rows, d), BF16),
                 pltpu.VMEM((rows, d), BF16),
-                dma((len(LOADS) + 1,)),
+                dma((2,)),
                 dma((2,)),
                 dma((chunks,)),
                 dma((2,)),

time: 94.5 us -> 94.4 us (level)
  no operation moved by 1% of the time
where the time goes in v7:
time: 94.4 us
  Pallas kernels  93 us (99%)
  local copies, waits for them, and re-layouts  1.32 us (1%)
    pallas_call x1, Pallas kernels, step(): pl.pallas_call(kernel, out_shape=pltpu.VMEM((rows, d), BF16), in_specs=[p...  93 us

profile of v7, /device:TPU:1, one launch (start us, length us, event | category | flops | bytes accessed | tf_op | source)
XLA Modules:
  0.0 94.4 jit_solution(9558143691970596720)
XLA Ops:
  0.0 93.0 %mlp_ring.1 = bf16[512,2048]{1,0:T(8,128)(2,1)S(1)} custom-call(bf16[512,2048]{1,0:T(8,128)(2,1)} %x.1, bf16[2048,2048]{1,0:T(8,128)(2,1)} %w_gate.1, bf16[2048,2048]{1,0:T(8,128)(2,1)} %w_up.1, bf16[2048,2048]{1,0:T(8,128)(2,1)} %w_down.1), custom_call_target="tpu_custom_call" | custom-call | tf_op jit(solution)/shard_map/mlp_ring/pallas_call | solution.py:290
  93.0 1.3 %copy.6 = bf16[512,2048]{1,0:T(8,128)(2,1)} copy(bf16[512,2048]{1,0:T(8,128)(2,1)S(1)} %mlp_ring.1) | data formatting | bytes 4194304

commit v8 on v7

--- a/solution.py
+++ b/solution.py
@@ -12,10 +12,11 @@
 M = 2 * HALF
 NT = 1024
 BLK = 32
-MOVED = 32
+MOVED = 48
 KEPT = HALF - MOVED
 PIECES = ((0, 0, HALF), (1, 0, HALF), (2, 0, HALF), (3, 0, KEPT), (3, KEPT, MOVED))
 LAST = 3
+ROUND = (16, 768)
 
 ORDER = (("L", 0), ("L", 1), ("R", 0), ("L", 2), ("R", 1), ("R", 2), ("L", 3), ("R", 3))
 SLOT = {k: s for s, k in enumerate(ORDER)}
@@ -26,12 +27,17 @@
 def kernel(
     x, w_gate, w_up, w_down, out,
     xs, wgu, wd, hid, term, local, to_sib, from_sib, to_far, from_far,
-    load, early, far_recv, fwd_recv, own_term, sum_recv, sent, sib_in,
+    load, early, far_recv, fwd_recv, own_term, sum_recv, sent, sib_in, relay, relay_sem,
 ):
     me = lax.axis_index("tp")
     core = lax.rem(me, 2)
     sib = me + 1 - 2 * core
     far = lax.rem(me + 2, 4)
+    dp, chip = lax.axis_index("dp"), lax.div(me, 2)
+    giver = (core == 0) & (dp == 0) & (chip == 1)
+    first_hop = (core == 0) & (dp == 1) & (chip == 1)
+    second_hop = (core == 0) & (dp == 1) & (chip == 0)
+    across = dp + chip - 2 * dp * chip
     steps = len(ORDER)
     tiles = wd.shape[0]
     chunks = x.shape[0] // HALF
@@ -88,6 +94,31 @@
         return remote(slab(("R", LAST), HALF + KEPT, MOVED), slab(("R", LAST), KEPT, MOVED),
                       sent, fwd_recv[LAST], sib)
 
+    round_rows = KEPT - ROUND[0]
+
+    def over_y(src, dst, send_sem, recv_sem):
+        return pltpu.make_async_remote_copy(
+            src_ref=src, dst_ref=dst, send_sem=send_sem, recv_sem=recv_sem,
+            device_id={"dp": 1 - dp}, device_id_type=MESH)
+
+    def give():
+        src = x.at[pl.ds(LAST * HALF + round_rows, ROUND[0]), pl.ds(0, ROUND[1])]
+        return over_y(src, relay.at[0], sent, relay_sem.at[0])
+
+    def relay_on():
+        return remote(relay.at[0], relay.at[1], load.at[0], relay_sem.at[0], far)
+
+    def hand_over():
+        dst = xs.at[pl.ds(SLOT["R", LAST] * M + round_rows, ROUND[0]), pl.ds(0, ROUND[1])]
+        return over_y(relay.at[1], dst, load.at[0], far_recv.at[LAST])
+
+    def not_given():
+        at, to = LAST * HALF, SLOT["R", LAST] * M
+        rest = pl.ds(ROUND[1], depth - ROUND[1])
+        return (remote(x.at[pl.ds(at, round_rows)], xs.at[pl.ds(to, round_rows)], sent, far_recv.at[LAST], far),
+                remote(x.at[pl.ds(at + round_rows, ROUND[0]), rest],
+                       xs.at[pl.ds(to + round_rows, ROUND[0]), rest], sent, far_recv.at[LAST], far))
+
     def term_copy(s):
         kind, i = ORDER[s]
         return remote(to_sib.at[s], from_sib.at[s], sent, term_recv[i if kind == "R" else chunks], sib)
@@ -104,17 +135,18 @@
     def _():
         pl.semaphore_signal(barrier, inc=1, device_id={"tp": sib}, device_id_type=MESH)
 
-    pl.semaphore_wait(barrier, 2 - core)
-    for p in range(LAST_PIECE):
+    @pl.when((core == 0) & (across == 0))
+    def _():
+        pl.semaphore_signal(barrier, inc=1, device_id={"dp": 1 - dp}, device_id_type=MESH)
+
+    pl.semaphore_wait(barrier, 2 - core + (1 - core) * across)
+    for p in range(2):
         to_far_chip(p).start()
+    when(giver, lambda: give().start())
 
     @pl.when(core == 0)
     def _():
         pl.semaphore_signal(sib_in, inc=1, device_id={"tp": sib}, device_id_type=MESH)
-
-    @pl.when(core == 1)
-    def _():
-        to_far_chip(LAST_PIECE).start()
 
     for j in range(chunks):
         own(j).start()
@@ -223,7 +255,32 @@
         def _():
             arrived(wd, load.at[1])
             arrived(xs.at[pl.ds(0, (chunks - 1) * HALF)], sib_recv[1])
-            when(core == 1, lambda: extra().start())
+
+            @pl.when(first_hop)
+            def _():
+                arrived(relay.at[0], relay_sem.at[0])
+                relay_on().start()
+
+            to_far_chip(2).start()
+
+            @pl.when(giver)
+            def _():
+                for c in not_given():
+                    c.start()
+
+            @pl.when(jnp.logical_not(giver))
+            def _():
+                to_far_chip(LAST).start()
+
+            @pl.when(core == 1)
+            def _():
+                to_far_chip(LAST_PIECE).start()
+                extra().start()
+
+        @pl.when((s == 3) & second_hop)
+        def _():
+            arrived(relay.at[1], relay_sem.at[0])
+            hand_over().start()
 
         for k in range(1, steps):
             if ORDER[k - 1][0] == "R":
@@ -266,6 +323,7 @@
         rows = pl.ds(i * HALF + r, n)
         out[rows] = (local[rows] + from_far[rows].astype(F32)).astype(BF16)
 
+    when(first_hop | second_hop, lambda: left(relay.at[0], load.at[0]))
     arrived(from_far.at[pl.ds(0, x.shape[0] - MOVED)], sum_recv.at[0])
     for p in range(LAST_PIECE):
         finish(p)
@@ -274,7 +332,7 @@
     rows = x.shape[0]
     for c, far_rows in enumerate((rows - MOVED, rows + MOVED)):
         total = 2 * (far_rows + rows) + steps * HALF
-        when(core == c, lambda: left(wgu.at[pl.ds(0, total * x.shape[1] // NT)], sent))
+        when(core == c, lambda: left(wgu.at[pl.ds(0, total * depth // NT)], sent))
 
 
 LAST_PIECE = len(PIECES) - 1
@@ -311,6 +369,8 @@
                 dma((2,)),
                 dma((1,)),
                 pltpu.SemaphoreType.REGULAR,
+                pltpu.VMEM((2, *ROUND), BF16),
+                dma((1,)),
             ],
             compiler_params=pltpu.CompilerParams(
                 collective_id=0, has_side_effects=True, vmem_limit_bytes=63000000),

time: 94.4 us -> 94.2 us (level)
  no operation moved by 1% of the time
where the time goes in v8:
time: 94.2 us; the launch traced here: 94.1 us
  Pallas kernels  92.8 us (99%)
  local copies, waits for them, and re-layouts  1.32 us (1%)
    pallas_call x1, Pallas kernels, step(): pl.pallas_call(kernel, out_shape=pltpu.VMEM((rows, d), BF16), in_specs=[p...  92.8 us

profile of v8, /device:TPU:1, one launch (start us, length us, event | category | flops | bytes accessed | tf_op | source)
XLA Modules:
  0.0 94.1 jit_solution(17427275304280437585)
XLA Ops:
  0.0 92.8 %mlp_ring.1 = bf16[512,2048]{1,0:T(8,128)(2,1)S(1)} custom-call(bf16[512,2048]{1,0:T(8,128)(2,1)} %x.1, bf16[2048,2048]{1,0:T(8,128)(2,1)} %w_gate.1, bf16[2048,2048]{1,0:T(8,128)(2,1)} %w_up.1, bf16[2048,2048]{1,0:T(8,128)(2,1)} %w_down.1), custom_call_target="tpu_custom_call" | custom-call | tf_op jit(solution)/shard_map/mlp_ring/pallas_call | solution.py:348
  92.8 1.3 %copy.6 = bf16[512,2048]{1,0:T(8,128)(2,1)} copy(bf16[512,2048]{1,0:T(8,128)(2,1)S(1)} %mlp_ring.1) | data formatting | bytes 4194304

commit v9 on v8

--- a/solution.py
+++ b/solution.py
@@ -15,6 +15,7 @@
 MOVED = 48
 KEPT = HALF - MOVED
 PIECES = ((0, 0, HALF), (1, 0, HALF), (2, 0, HALF), (3, 0, KEPT), (3, KEPT, MOVED))
+TERMS_AT = {3: (0, 1, 2), 4: (3,), 5: (4,), 6: (5,), 7: (6,)}
 LAST = 3
 ROUND = (16, 768)
 
@@ -27,7 +28,7 @@
 def kernel(
     x, w_gate, w_up, w_down, out,
     xs, wgu, wd, hid, term, local, to_sib, from_sib, to_far, from_far,
-    load, early, far_recv, fwd_recv, own_term, sum_recv, sent, sib_in, relay, relay_sem,
+    load, early, far_recv, fwd_recv, sum_recv, sent, relay, relay_sem,
 ):
     me = lax.axis_index("tp")
     core = lax.rem(me, 2)
@@ -44,8 +45,8 @@
     depth = x.shape[1]
     sent = sent.at[0]
     sib_recv = (early.at[0], early.at[1])
-    fwd_recv = (fwd_recv.at[0], fwd_recv.at[1], early.at[0], early.at[1])
-    term_recv = tuple(far_recv.at[i] for i in range(4)) + (own_term.at[0],)
+    fwd_recv = (fwd_recv.at[0], early.at[0], early.at[1], early.at[0])
+    term_recv = tuple(far_recv.at[i] for i in range(4)) + (load.at[1],)
 
     def when(c, f):
         pl.when(c)(f)
@@ -146,22 +147,22 @@
 
     @pl.when(core == 0)
     def _():
-        pl.semaphore_signal(sib_in, inc=1, device_id={"tp": sib}, device_id_type=MESH)
+        for j in range(chunks):
+            to_sibling(j).start()
 
     for j in range(chunks):
         own(j).start()
     for n in range(tiles):
         for c in weights(n):
             c.start()
+    for n in range(tiles):
+        weights_down(n).start()
+    arrived(xs.at[pl.ds(0, x.shape[0] + HALF)], sib_recv[0])
 
     @pl.when(core == 1)
     def _():
-        pl.semaphore_wait(sib_in, 1)
-
-    for j in range(chunks):
-        to_sibling(j).start()
-    for n in range(tiles):
-        weights_down(n).start()
+        for j in range(chunks):
+            to_sibling(j).start()
 
     def pass_on(i):
         if i != LAST:
@@ -185,7 +186,6 @@
         kind, i = ORDER[k]
         if kind == "L":
             if i == 0:
-                arrived(xs.at[pl.ds(0, x.shape[0] + HALF)], sib_recv[0])
                 arrived(wgu, load.at[0])
         elif i != LAST:
             arrived(slab(("R", i), HALF, HALF), fwd_recv[i])
@@ -246,7 +246,8 @@
             hid[:, pl.ds(pl.multiple_of(n * NT, NT), NT)] = (jax.nn.silu(gate) * up).astype(BF16)
 
             for k in range(1, steps):
-                when((s == k) & (n == 0), lambda: term_copy(k - 1).start())
+                for t in TERMS_AT.get(k, ()):
+                    when((s == k) & (n == 0), lambda: term_copy(t).start())
             return 0
 
         lax.fori_loop(0, tiles, gate_up, 0)
@@ -364,11 +365,9 @@
                 dma((2,)),
                 dma((2,)),
                 dma((chunks,)),
-                dma((2,)),
                 dma((1,)),
                 dma((2,)),
                 dma((1,)),
-                pltpu.SemaphoreType.REGULAR,
                 pltpu.VMEM((2, *ROUND), BF16),
                 dma((1,)),
             ],

time: 94.2 us -> 94.2 us (level)
  no operation moved by 1% of the time
where the time goes in v9:
time: 94.2 us; the launch traced here: 94.1 us
  Pallas kernels  92.8 us (99%)
  local copies, waits for them, and re-layouts  1.32 us (1%)
    pallas_call x1, Pallas kernels, step(): pl.pallas_call(kernel, out_shape=pltpu.VMEM((rows, d), BF16), in_specs=[p...  92.8 us

profile of v9, /device:TPU:1, one launch (start us, length us, event | category | flops | bytes accessed | tf_op | source)
XLA Modules:
  0.0 94.1 jit_solution(12666192587445005982)
XLA Ops:
  0.0 92.8 %mlp_ring.1 = bf16[512,2048]{1,0:T(8,128)(2,1)S(1)} custom-call(bf16[512,2048]{1,0:T(8,128)(2,1)} %x.1, bf16[2048,2048]{1,0:T(8,128)(2,1)} %w_gate.1, bf16[2048,2048]{1,0:T(8,128)(2,1)} %w_up.1, bf16[2048,2048]{1,0:T(8,128)(2,1)} %w_down.1), custom_call_target="tpu_custom_call" | custom-call | tf_op jit(solution)/shard_map/mlp_ring/pallas_call | solution.py:349
  92.8 1.3 %copy.6 = bf16[512,2048]{1,0:T(8,128)(2,1)} copy(bf16[512,2048]{1,0:T(8,128)(2,1)S(1)} %mlp_ring.1) | data formatting | bytes 4194304

commit v10 on v9

--- a/solution.py
+++ b/solution.py
@@ -66,7 +66,7 @@
         return xs.at[pl.ds(SLOT[key] * M + first, n)]
 
     def own(j):
-        return pltpu.make_async_copy(x.at[pl.ds(j * HALF, HALF)], slab(("L", j), 0, HALF), sib_recv[0])
+        return pltpu.make_async_copy(x.at[pl.ds(j * HALF, HALF)], slab(("L", j), 0, HALF), load.at[0])
 
     def weights(n):
         c = pl.ds(n * NT, NT)
@@ -157,7 +157,7 @@
             c.start()
     for n in range(tiles):
         weights_down(n).start()
-    arrived(xs.at[pl.ds(0, x.shape[0] + HALF)], sib_recv[0])
+    arrived(xs.at[pl.ds(0, HALF)], sib_recv[0])
 
     @pl.when(core == 1)
     def _():
@@ -186,7 +186,9 @@
         kind, i = ORDER[k]
         if kind == "L":
             if i == 0:
+                arrived(xs.at[pl.ds(0, (chunks - 1) * HALF)], sib_recv[1])
                 arrived(wgu, load.at[0])
+                arrived(xs.at[pl.ds(0, x.shape[0])], load.at[0])
         elif i != LAST:
             arrived(slab(("R", i), HALF, HALF), fwd_recv[i])
         else:
@@ -255,7 +257,6 @@
         @pl.when(s == 0)
         def _():
             arrived(wd, load.at[1])
-            arrived(xs.at[pl.ds(0, (chunks - 1) * HALF)], sib_recv[1])
 
             @pl.when(first_hop)
             def _():

time: 94.2 us -> 94.2 us (level)
  no operation moved by 1% of the time
where the time goes in v10:
time: 94.2 us; the launch traced here: 94.1 us
  Pallas kernels  92.8 us (99%)
  local copies, waits for them, and re-layouts  1.32 us (1%)
    pallas_call x1, Pallas kernels, step(): pl.pallas_call(kernel, out_shape=pltpu.VMEM((rows, d), BF16), in_specs=[p...  92.8 us

profile of v10, /device:TPU:1, one launch (start us, length us, event | category | flops | bytes accessed | tf_op | source)
XLA Modules:
  0.0 94.1 jit_solution(5221015733460795660)
XLA Ops:
  0.0 92.8 %mlp_ring.1 = bf16[512,2048]{1,0:T(8,128)(2,1)S(1)} custom-call(bf16[512,2048]{1,0:T(8,128)(2,1)} %x.1, bf16[2048,2048]{1,0:T(8,128)(2,1)} %w_gate.1, bf16[2048,2048]{1,0:T(8,128)(2,1)} %w_up.1, bf16[2048,2048]{1,0:T(8,128)(2,1)} %w_down.1), custom_call_target="tpu_custom_call" | custom-call | tf_op jit(solution)/shard_map/mlp_ring/pallas_call | solution.py:350
  92.8 1.3 %copy.6 = bf16[512,2048]{1,0:T(8,128)(2,1)} copy(bf16[512,2048]{1,0:T(8,128)(2,1)S(1)} %mlp_ring.1) | data formatting | bytes 4194304

commit v11 on v9

--- a/solution.py
+++ b/solution.py
@@ -16,6 +16,7 @@
 KEPT = HALF - MOVED
 PIECES = ((0, 0, HALF), (1, 0, HALF), (2, 0, HALF), (3, 0, KEPT), (3, KEPT, MOVED))
 TERMS_AT = {3: (0, 1, 2), 4: (3,), 5: (4,), 6: (5,), 7: (6,)}
+SUMS = ((0, 0, HALF), (1, 0, HALF), (2, 0, HALF), (3, 0, HALF - 16), (3, HALF - 16, 16))
 LAST = 3
 ROUND = (16, 768)
 
@@ -28,7 +29,7 @@
 def kernel(
     x, w_gate, w_up, w_down, out,
     xs, wgu, wd, hid, term, local, to_sib, from_sib, to_far, from_far,
-    load, early, far_recv, fwd_recv, sum_recv, sent, relay, relay_sem,
+    load, early, far_recv, sum_first, sent, relay, relay_sem,
 ):
     me = lax.axis_index("tp")
     core = lax.rem(me, 2)
@@ -45,8 +46,9 @@
     depth = x.shape[1]
     sent = sent.at[0]
     sib_recv = (early.at[0], early.at[1])
-    fwd_recv = (fwd_recv.at[0], early.at[0], early.at[1], early.at[0])
+    fwd_recv = (early.at[0], early.at[1], early.at[0], early.at[1])
     term_recv = tuple(far_recv.at[i] for i in range(4)) + (load.at[1],)
+    sum_recv = (sum_first.at[0], load.at[0])
 
     def when(c, f):
         pl.when(c)(f)
@@ -107,11 +109,11 @@
         return over_y(src, relay.at[0], sent, relay_sem.at[0])
 
     def relay_on():
-        return remote(relay.at[0], relay.at[1], load.at[0], relay_sem.at[0], far)
+        return remote(relay.at[0], relay.at[1], relay_sem.at[0], relay_sem.at[0], far)
 
     def hand_over():
         dst = xs.at[pl.ds(SLOT["R", LAST] * M + round_rows, ROUND[0]), pl.ds(0, ROUND[1])]
-        return over_y(relay.at[1], dst, load.at[0], far_recv.at[LAST])
+        return over_y(relay.at[1], dst, relay_sem.at[0], far_recv.at[LAST])
 
     def not_given():
         at, to = LAST * HALF, SLOT["R", LAST] * M
@@ -125,9 +127,9 @@
         return remote(to_sib.at[s], from_sib.at[s], sent, term_recv[i if kind == "R" else chunks], sib)
 
     def sum_copy(p):
-        i, r, n = PIECES[p]
+        i, r, n = SUMS[p]
         rows = pl.ds(i * HALF + r, n)
-        return remote(to_far.at[rows], from_far.at[rows], sent, sum_recv.at[p // LAST_PIECE], far)
+        return remote(to_far.at[rows], from_far.at[rows], sent, sum_recv[p // LAST_PIECE], far)
 
     barrier = pltpu.get_barrier_semaphore()
     pl.semaphore_signal(barrier, inc=1, device_id={"tp": far}, device_id_type=MESH)
@@ -145,11 +147,7 @@
         to_far_chip(p).start()
     when(giver, lambda: give().start())
 
-    @pl.when(core == 0)
-    def _():
-        for j in range(chunks):
-            to_sibling(j).start()
-
+    when(core == 0, lambda: to_sibling(0).start())
     for j in range(chunks):
         own(j).start()
     for n in range(tiles):
@@ -159,10 +157,9 @@
         weights_down(n).start()
     arrived(xs.at[pl.ds(0, x.shape[0] + HALF)], sib_recv[0])
 
-    @pl.when(core == 1)
-    def _():
-        for j in range(chunks):
-            to_sibling(j).start()
+    when(core == 1, lambda: to_sibling(0).start())
+    for j in range(1, chunks):
+        to_sibling(j).start()
 
     def pass_on(i):
         if i != LAST:
@@ -230,7 +227,7 @@
         blocks(HALF, blk)
 
     def start_sum(k):
-        for p, (i, _, _) in enumerate(PIECES):
+        for p, (i, _, _) in enumerate(SUMS):
             if i == ORDER[k][1]:
                 sum_copy(p).start()
 
@@ -320,15 +317,15 @@
     start_sum(last)
 
     def finish(p):
-        i, r, n = PIECES[p]
+        i, r, n = SUMS[p]
         rows = pl.ds(i * HALF + r, n)
         out[rows] = (local[rows] + from_far[rows].astype(F32)).astype(BF16)
 
-    when(first_hop | second_hop, lambda: left(relay.at[0], load.at[0]))
-    arrived(from_far.at[pl.ds(0, x.shape[0] - MOVED)], sum_recv.at[0])
+    when(first_hop | second_hop, lambda: left(relay.at[0], relay_sem.at[0]))
+    arrived(from_far.at[pl.ds(0, x.shape[0] - SUMS[-1][2])], sum_recv[0])
     for p in range(LAST_PIECE):
         finish(p)
-    arrived(from_far.at[pl.ds(0, MOVED)], sum_recv.at[1])
+    arrived(from_far.at[pl.ds(0, SUMS[-1][2])], sum_recv[1])
     finish(LAST_PIECE)
     rows = x.shape[0]
     for c, far_rows in enumerate((rows - MOVED, rows + MOVED)):
@@ -366,7 +363,6 @@
                 dma((2,)),
                 dma((chunks,)),
                 dma((1,)),
-                dma((2,)),
                 dma((1,)),
                 pltpu.VMEM((2, *ROUND), BF16),
                 dma((1,)),

time: 94.2 us -> 94.1 us (level)
  no operation moved by 1% of the time
where the time goes in v11:
time: 94.1 us
  Pallas kernels  92.7 us (99%)
  local copies, waits for them, and re-layouts  1.32 us (1%)
    pallas_call x1, Pallas kernels, step(): pl.pallas_call(kernel, out_shape=pltpu.VMEM((rows, d), BF16), in_specs=[p...  92.7 us

profile of v11, /device:TPU:1, one launch (start us, length us, event | category | flops | bytes accessed | tf_op | source)
XLA Modules:
  0.0 94.1 jit_solution(6176767055283288663)
XLA Ops:
  0.0 92.7 %mlp_ring.1 = bf16[512,2048]{1,0:T(8,128)(2,1)S(1)} custom-call(bf16[512,2048]{1,0:T(8,128)(2,1)} %x.1, bf16[2048,2048]{1,0:T(8,128)(2,1)} %w_gate.1, bf16[2048,2048]{1,0:T(8,128)(2,1)} %w_up.1, bf16[2048,2048]{1,0:T(8,128)(2,1)} %w_down.1), custom_call_target="tpu_custom_call" | custom-call | tf_op jit(solution)/shard_map/mlp_ring/pallas_call | solution.py:346
  92.7 1.3 %copy.6 = bf16[512,2048]{1,0:T(8,128)(2,1)} copy(bf16[512,2048]{1,0:T(8,128)(2,1)S(1)} %mlp_ring.1) | data formatting | bytes 4194304
